TPU v7x, 32 devices: a whole 2x2x4 slice. The times are simulated.
32 devices in a mesh: dp: 8 (over y, x, core), tensor: 4 (over z).
Axes of the slice: x: 2, y: 2, z: 4, core: 2. Of those that a mesh axis runs over, the one named last changes fastest.
Arguments:
- tokens: bfloat16 [4096, 1024], P(('dp', 'tensor')), may hold values from -5 to 5
- lengths: int32 [8, 2], P('dp'), may hold values from 0 to 512, as said below
- w_query: bfloat16 [1024, 1024], P('dp', 'tensor'), may hold values from -0.1875 to 0.1875
- b_query: float32 [1024], replicated, may hold values from -3 to 3
- w_key: bfloat16 [1024, 1024], P('dp', 'tensor'), may hold values from -0.1875 to 0.1875
- w_value: bfloat16 [1024, 1024], P('dp', 'tensor'), may hold values from -0.1875 to 0.1875
- b_value: float32 [1024], replicated, may hold values from -3 to 3
- w_out: bfloat16 [1024, 1024], P('tensor', 'dp'), may hold values from -3 to 3
- b_out: float32 [1024], replicated, may hold values from -3 to 3
- gain_attn: float32 [1024], replicated, may hold values from 0.1 to 1.9
- shift_attn: float32 [1024], replicated, may hold values from -3 to 3
- w_in: bfloat16 [1024, 4096], P('dp', 'tensor'), may hold values from -0.1875 to 0.1875
- b_in: float32 [4096], replicated, may hold values from -3 to 3
- w_back: bfloat16 [4096, 1024], P('tensor', 'dp'), may hold values from -0.09375 to 0.09375
- b_back: float32 [1024], replicated, may hold values from -3 to 3
- gain_ffn: float32 [1024], replicated, may hold values from 0.1 to 1.9
- shift_ffn: float32 [1024], replicated, may hold values from -3 to 3
- cotangent: bfloat16 [4096, 1024], P(('dp', 'tensor')), may hold values from -6 to 6
Outputs:
- output: bfloat16 [4096, 1024], P(('dp', 'tensor'))
- grad_tokens: float32 [4096, 1024], P(('dp', 'tensor'))
- grad_w_query: float32 [1024, 1024], P('dp', 'tensor')
- grad_b_query: float32 [1024], replicated
- grad_w_key: float32 [1024, 1024], P('dp', 'tensor')
- grad_w_value: float32 [1024, 1024], P('dp', 'tensor')
- grad_b_value: float32 [1024], replicated
- grad_w_out: float32 [1024, 1024], P('tensor', 'dp')
- grad_b_out: float32 [1024], replicated
- grad_gain_attn: float32 [1024], replicated
- grad_shift_attn: float32 [1024], replicated
- grad_w_in: float32 [1024, 4096], P('dp', 'tensor')
- grad_b_in: float32 [4096], replicated
- grad_w_back: float32 [4096, 1024], P('tensor', 'dp')
- grad_b_back: float32 [1024], replicated
- grad_gain_ffn: float32 [1024], replicated
- grad_shift_ffn: float32 [1024], replicated
Inputs may be any that keep to these rules, and one draw needn't show every extreme that they name: Each group's 2 lengths sum to at most 512; the first is 1 or more, the second may be 0; in every draw one group holds a single sequence of exactly 512 tokens.
All inputs are finite; a program needn't handle non-finite values.
Results may differ from a plain program's by a relative error of at most 0.02.
Values may be sent and summed in bfloat16 or wider, within the bound.
A program may use at most 128 MiB of HBM per device.

v0:
```python
import jax
import jax.numpy as jnp
from jax import lax
from jax.sharding import PartitionSpec as P

HD = 64
epsilon = 1e-06
masked_value = -1e30


def matmul_plain(left_side, right_side):
    return jnp.dot(left_side, right_side, preferred_element_type=jnp.float32)


def matmul_over_rows(left_side, right_side):
    return lax.dot_general(
        left_side, right_side, (((0,), (0,)), ((), ())), preferred_element_type=jnp.float32
    )


def matmul_over_cols(left_side, right_side):
    return lax.dot_general(
        left_side, right_side, (((1,), (1,)), ((), ())), preferred_element_type=jnp.float32
    )


def layer_norm(residual, gain_vec, shift_vec):
    mean_val = jnp.mean(residual, axis=-1, keepdims=True)
    centered = residual - mean_val
    inv_std = lax.rsqrt(jnp.mean(centered * centered, axis=-1, keepdims=True) + epsilon)
    normed = centered * inv_std
    return (normed * gain_vec + shift_vec, normed, inv_std)


def norm_back(grad_out, normed, inv_std, gain_vec):
    grad_norm = grad_out * gain_vec
    first_mean = jnp.mean(grad_norm, axis=-1, keepdims=True)
    second_mean = jnp.mean(grad_norm * normed, axis=-1, keepdims=True)
    return inv_std * (grad_norm - first_mean - normed * second_mean)


def gelu_parts(preact):
    cdf_val = 0.5 * (1.0 + lax.erf(preact * 0.7071067811865476))
    pdf_val = jnp.exp(-0.5 * preact * preact) * 0.3989422804014327
    return (preact * cdf_val, cdf_val + preact * pdf_val)


def attend_forward(query_rows, key_rows, value_rows, seg_ids, head_dim, block_rows):
    group_rows, head_cols = query_rows.shape
    pair_width = 2 * head_dim
    block_count = group_rows // block_rows
    pair_count = head_cols // pair_width
    score_scale = head_dim ** (-0.5)

    def attend_step(step_index, loop_carry):
        context, log_total = loop_carry
        pair_index = step_index // block_count
        row_start = step_index % block_count * block_rows
        first_col = pair_index * pair_width
        query_block = lax.dynamic_slice(
            query_rows, (row_start, first_col), (block_rows, pair_width)
        ).reshape(block_rows, 2, head_dim)
        key_pair = lax.dynamic_slice(key_rows, (0, first_col), (group_rows, pair_width)).reshape(
            group_rows, 2, head_dim
        )
        value_pair = lax.dynamic_slice(
            value_rows, (0, first_col), (group_rows, pair_width)
        ).reshape(group_rows, 2, head_dim)
        same_seg = seg_ids[:, None] == seg_ids[None, :]
        scores = (
            jnp.einsum("qhd,khd->hqk", query_block, key_pair, preferred_element_type=jnp.float32)
            * score_scale
        )
        scores = jnp.where(same_seg[None], scores, masked_value)
        row_max = jnp.max(scores, axis=-1, keepdims=True)
        block_total = row_max + jnp.log(jnp.sum(jnp.exp(scores - row_max), axis=-1, keepdims=True))
        prob_bf = jnp.exp(scores - block_total).astype(jnp.bfloat16)
        context_block = jnp.einsum(
            "hqk,khd->qhd", prob_bf, value_pair, preferred_element_type=jnp.float32
        ).astype(jnp.bfloat16)
        context = lax.dynamic_update_slice(
            context, context_block.reshape(block_rows, pair_width), (row_start, first_col)
        )
        log_total = lax.dynamic_update_slice(
            log_total, block_total[:, :, 0], (2 * pair_index, row_start)
        )
        return (context, log_total)

    start_carry = (
        jnp.zeros((group_rows, head_cols), jnp.bfloat16),
        jnp.zeros((head_cols // head_dim, group_rows), jnp.float32),
    )
    return lax.fori_loop(0, pair_count * block_count, attend_step, start_carry)


def attend_backward(
    query_rows,
    key_rows,
    value_rows,
    context,
    grad_context,
    log_total,
    seg_ids,
    head_dim,
    block_rows,
):
    group_rows, head_cols = query_rows.shape
    pair_width = 2 * head_dim
    block_count = group_rows // block_rows
    pair_count = head_cols // pair_width
    score_scale = head_dim ** (-0.5)

    def back_step(step_index, loop_carry):
        grad_query, grad_keys, grad_values = loop_carry
        pair_index = step_index // block_count
        row_start = step_index % block_count * block_rows
        first_col = pair_index * pair_width
        query_block = lax.dynamic_slice(
            query_rows, (row_start, first_col), (block_rows, pair_width)
        ).reshape(block_rows, 2, head_dim)
        key_pair = lax.dynamic_slice(key_rows, (0, first_col), (group_rows, pair_width)).reshape(
            group_rows, 2, head_dim
        )
        value_pair = lax.dynamic_slice(
            value_rows, (0, first_col), (group_rows, pair_width)
        ).reshape(group_rows, 2, head_dim)
        context_block = lax.dynamic_slice(
            context, (row_start, first_col), (block_rows, pair_width)
        ).reshape(block_rows, 2, head_dim)
        gctx_block = lax.dynamic_slice(
            grad_context, (row_start, first_col), (block_rows, pair_width)
        ).reshape(block_rows, 2, head_dim)
        total_block = lax.dynamic_slice(log_total, (2 * pair_index, row_start), (2, block_rows))
        same_seg = seg_ids[:, None] == seg_ids[None, :]
        scores = (
            jnp.einsum("qhd,khd->hqk", query_block, key_pair, preferred_element_type=jnp.float32)
            * score_scale
        )
        scores = jnp.where(same_seg[None], scores, masked_value)
        probs = jnp.exp(scores - total_block[:, :, None])
        prob_bf = probs.astype(jnp.bfloat16)
        grad_probs = jnp.einsum(
            "qhd,khd->hqk", gctx_block, value_pair, preferred_element_type=jnp.float32
        )
        delta_rows = jnp.sum(
            gctx_block.astype(jnp.float32) * context_block.astype(jnp.float32), axis=-1
        ).T[:, :, None]
        grad_scores = (probs * (grad_probs - delta_rows) * score_scale).astype(jnp.bfloat16)
        grad_q_block = jnp.einsum(
            "hqk,khd->qhd", grad_scores, key_pair, preferred_element_type=jnp.float32
        ).reshape(block_rows, pair_width)
        grad_k_pair = jnp.einsum(
            "hqk,qhd->khd", grad_scores, query_block, preferred_element_type=jnp.float32
        ).reshape(group_rows, pair_width)
        grad_v_pair = jnp.einsum(
            "hqk,qhd->khd", prob_bf, gctx_block, preferred_element_type=jnp.float32
        ).reshape(group_rows, pair_width)
        grad_query = lax.dynamic_update_slice(grad_query, grad_q_block, (row_start, first_col))
        old_keys = lax.dynamic_slice(grad_keys, (0, first_col), (group_rows, pair_width))
        grad_keys = lax.dynamic_update_slice(grad_keys, old_keys + grad_k_pair, (0, first_col))
        old_values = lax.dynamic_slice(grad_values, (0, first_col), (group_rows, pair_width))
        grad_values = lax.dynamic_update_slice(
            grad_values, old_values + grad_v_pair, (0, first_col)
        )
        return (grad_query, grad_keys, grad_values)

    zero_grad = jnp.zeros((group_rows, head_cols), jnp.float32)
    return lax.fori_loop(0, pair_count * block_count, back_step, (zero_grad, zero_grad, zero_grad))


def on_device(
    tokens,
    lengths,
    w_query,
    b_query,
    w_key,
    w_value,
    b_value,
    w_out,
    b_out,
    gain_attn,
    shift_attn,
    w_in,
    b_in,
    w_back,
    b_back,
    gain_ffn,
    shift_ffn,
    cotangent,
):
    tensor_size = lax.axis_size("tensor")
    tensor_index = lax.axis_index("tensor")
    local_rows = tokens.shape[0]
    group_rows = local_rows * tensor_size
    head_cols = w_query.shape[1]
    hidden_cols = w_in.shape[1]
    block_rows = min(512, group_rows)
    seq_lens = lengths[0]
    live_end = seq_lens[0] + seq_lens[1]
    positions = jnp.arange(group_rows, dtype=jnp.int32)
    seg_ids = (positions >= seq_lens[0]).astype(jnp.int32) + (positions >= live_end).astype(
        jnp.int32
    )
    local_pos = tensor_index * local_rows + jnp.arange(local_rows, dtype=jnp.int32)
    live_rows = (local_pos < live_end).astype(jnp.float32)[:, None]
    rows_full = lax.all_gather(tokens, "tensor", axis=0, tiled=True)
    attn_mats = (
        lax.all_gather(w_query, "dp", axis=0, tiled=True),
        lax.all_gather(w_key, "dp", axis=0, tiled=True),
        lax.all_gather(w_value, "dp", axis=0, tiled=True),
        lax.all_gather(w_out, "dp", axis=1, tiled=True),
    )
    mat_query, mat_key, mat_value, mat_out = attn_mats
    bias_query = lax.dynamic_slice_in_dim(b_query, tensor_index * head_cols, head_cols)
    bias_value = lax.dynamic_slice_in_dim(b_value, tensor_index * head_cols, head_cols)
    bias_in = lax.dynamic_slice_in_dim(b_in, tensor_index * hidden_cols, hidden_cols)
    query_rows = (matmul_plain(rows_full, mat_query) + bias_query).astype(jnp.bfloat16)
    key_rows = matmul_plain(rows_full, mat_key).astype(jnp.bfloat16)
    value_rows = (matmul_plain(rows_full, mat_value) + bias_value).astype(jnp.bfloat16)
    context, log_total = attend_forward(query_rows, key_rows, value_rows, seg_ids, HD, block_rows)
    attn_sum = lax.psum_scatter(
        matmul_plain(context, mat_out).astype(jnp.bfloat16),
        "tensor",
        scatter_dimension=0,
        tiled=True,
    ).astype(jnp.float32)
    resid_one = tokens.astype(jnp.float32) + attn_sum + b_out
    hidden_one, normed_one, inv_one = layer_norm(resid_one, gain_attn, shift_attn)
    hidden_bf = hidden_one.astype(jnp.bfloat16)
    hidden_full = lax.all_gather(hidden_bf, "tensor", axis=0, tiled=True)
    ffn_mats = (
        lax.all_gather(w_in, "dp", axis=0, tiled=True),
        lax.all_gather(w_back, "dp", axis=1, tiled=True),
    )
    mat_in, mat_back = ffn_mats
    preact = matmul_plain(hidden_full, mat_in) + bias_in
    activ_val, gelu_slope = gelu_parts(preact)
    activation = activ_val.astype(jnp.bfloat16)
    ffn_sum = lax.psum_scatter(
        matmul_plain(activation, mat_back).astype(jnp.bfloat16),
        "tensor",
        scatter_dimension=0,
        tiled=True,
    ).astype(jnp.float32)
    resid_two = hidden_one + ffn_sum + b_back
    normed_out, normed_two, inv_two = layer_norm(resid_two, gain_ffn, shift_ffn)
    output = (normed_out * live_rows).astype(jnp.bfloat16)
    grad_final = cotangent.astype(jnp.float32) * live_rows
    grad_gain_ffn = jnp.sum(grad_final * normed_two, axis=0)
    grad_shift_ffn = jnp.sum(grad_final, axis=0)
    grad_two = norm_back(grad_final, normed_two, inv_two, gain_ffn)
    grad_b_back = jnp.sum(grad_two, axis=0)
    mat_query, mat_key, mat_value, mat_out, mat_in, mat_back = (
        lax.all_gather(w_query, "dp", axis=0, tiled=True),
        lax.all_gather(w_key, "dp", axis=0, tiled=True),
        lax.all_gather(w_value, "dp", axis=0, tiled=True),
        lax.all_gather(w_out, "dp", axis=1, tiled=True),
        lax.all_gather(w_in, "dp", axis=0, tiled=True),
        lax.all_gather(w_back, "dp", axis=1, tiled=True),
    )
    grad_two_full = lax.all_gather(grad_two.astype(jnp.bfloat16), "tensor", axis=0, tiled=True)
    grad_w_back = matmul_over_rows(activation, grad_two_full)
    grad_pre = matmul_over_cols(grad_two_full, mat_back) * gelu_slope
    grad_b_in_part = jnp.sum(grad_pre, axis=0)
    grad_pre_bf = grad_pre.astype(jnp.bfloat16)
    grad_w_in = matmul_over_rows(hidden_full, grad_pre_bf)
    grad_one_out = grad_two + lax.psum_scatter(
        matmul_over_cols(grad_pre_bf, mat_in).astype(jnp.bfloat16),
        "tensor",
        scatter_dimension=0,
        tiled=True,
    ).astype(jnp.float32)
    grad_w_in, grad_w_back = (
        lax.psum_scatter(grad_w_in, "dp", scatter_dimension=0, tiled=True),
        lax.psum_scatter(grad_w_back, "dp", scatter_dimension=1, tiled=True),
    )
    grad_gain_attn = jnp.sum(grad_one_out * normed_one, axis=0)
    grad_shift_attn = jnp.sum(grad_one_out, axis=0)
    grad_one = norm_back(grad_one_out, normed_one, inv_one, gain_attn)
    grad_b_out = jnp.sum(grad_one, axis=0)
    grad_one_full = lax.all_gather(grad_one.astype(jnp.bfloat16), "tensor", axis=0, tiled=True)
    grad_w_out = matmul_over_rows(context, grad_one_full)
    grad_context = matmul_over_cols(grad_one_full, mat_out).astype(jnp.bfloat16)
    grad_query, grad_keys, grad_values = attend_backward(
        query_rows, key_rows, value_rows, context, grad_context, log_total, seg_ids, HD, block_rows
    )
    grad_b_query_part = jnp.sum(grad_query, axis=0)
    grad_b_value_part = jnp.sum(grad_values, axis=0)
    grad_query_bf = grad_query.astype(jnp.bfloat16)
    grad_keys_bf = grad_keys.astype(jnp.bfloat16)
    grad_values_bf = grad_values.astype(jnp.bfloat16)
    grad_w_query = matmul_over_rows(rows_full, grad_query_bf)
    grad_w_key = matmul_over_rows(rows_full, grad_keys_bf)
    grad_w_value = matmul_over_rows(rows_full, grad_values_bf)
    query_part = matmul_over_cols(grad_query_bf, mat_query)
    key_part = matmul_over_cols(grad_keys_bf, mat_key)
    value_part = matmul_over_cols(grad_values_bf, mat_value)
    grad_in = grad_one + lax.psum_scatter(
        (query_part + key_part + value_part).astype(jnp.bfloat16),
        "tensor",
        scatter_dimension=0,
        tiled=True,
    ).astype(jnp.float32)
    grad_w_query, grad_w_key, grad_w_value, grad_w_out = (
        lax.psum_scatter(grad_w_query, "dp", scatter_dimension=0, tiled=True),
        lax.psum_scatter(grad_w_key, "dp", scatter_dimension=0, tiled=True),
        lax.psum_scatter(grad_w_value, "dp", scatter_dimension=0, tiled=True),
        lax.psum_scatter(grad_w_out, "dp", scatter_dimension=1, tiled=True),
    )

    def widen(part_vec, full_width):
        return lax.dynamic_update_slice_in_dim(
            jnp.zeros((full_width,), jnp.float32), part_vec, tensor_index * part_vec.shape[0], 0
        )

    small_sums = lax.psum(
        (
            widen(grad_b_query_part, b_query.shape[0]),
            widen(grad_b_value_part, b_value.shape[0]),
            grad_b_out,
            grad_gain_attn,
            grad_shift_attn,
            widen(grad_b_in_part, b_in.shape[0]),
            grad_b_back,
            grad_gain_ffn,
            grad_shift_ffn,
        ),
        ("dp", "tensor"),
    )
    return (
        output,
        grad_in,
        grad_w_query,
        small_sums[0],
        grad_w_key,
        grad_w_value,
        small_sums[1],
        grad_w_out,
        small_sums[2],
        small_sums[3],
        small_sums[4],
        grad_w_in,
        small_sums[5],
        grad_w_back,
        small_sums[6],
        small_sums[7],
        small_sums[8],
    )


def solution(mesh):
    placed = (
        P(("dp", "tensor"), None),
        P("dp", None),
        P("dp", "tensor"),
        P(),
        P("dp", "tensor"),
        P("dp", "tensor"),
        P(),
        P("tensor", "dp"),
        P(),
        P(),
        P(),
        P("dp", "tensor"),
        P(),
        P("tensor", "dp"),
        P(),
        P(),
        P(),
        P(("dp", "tensor"), None),
    )
    return jax.shard_map(
        on_device,
        mesh=mesh,
        in_specs=placed,
        out_specs=(
            P(("dp", "tensor"), None),
            P(("dp", "tensor"), None),
            P("dp", "tensor"),
            P(),
            P("dp", "tensor"),
            P("dp", "tensor"),
            P(),
            P("tensor", "dp"),
            P(),
            P(),
            P(),
            P("dp", "tensor"),
            P(),
            P("tensor", "dp"),
            P(),
            P(),
            P(),
        ),
        check_vma=False,
    )
```

profile of v0, /device:TPU:0, one launch (start us, length us, event | category | flops | bytes accessed | tf_op | source)
XLA Modules:
  0.0 598.6 jit_solution(13437722508312491656)
XLA Ops:
  13.0 11.6 %all_gather.37 = bf16[1024,256]{1,0:T(8,128)(2,1)S(1)} all-gather(bf16[128,256]{1,0:T(8,128)(2,1)} %param.27), channel_id=1, replica_groups=mesh['dp'=8,'tensor'=4] {'dp'}, dimensions={0}, use_global_device_ids=true | all-gather | bytes 589824 | tf_op jit(solution)/shard_map/all_gather | solution.py:210
  24.6 9.5 %all_gather.38 = bf16[1024,256]{1,0:T(8,128)(2,1)S(1)} all-gather(bf16[128,256]{1,0:T(8,128)(2,1)} %param.24), channel_id=1, replica_groups=mesh['dp'=8,'tensor'=4] {'dp'}, dimensions={0}, use_global_device_ids=true | all-gather | bytes 589824 | tf_op jit(solution)/shard_map/all_gather | solution.py:208
  34.1 9.2 %all_gather.39 = bf16[1024,256]{1,0:T(8,128)(2,1)S(1)} all-gather(bf16[128,256]{1,0:T(8,128)(2,1)} %param.26), channel_id=1, replica_groups=mesh['dp'=8,'tensor'=4] {'dp'}, dimensions={0}, use_global_device_ids=true | all-gather | bytes 589824 | tf_op jit(solution)/shard_map/all_gather | solution.py:209
  43.3 10.6 %all_gather.40 = bf16[256,1024]{1,0:T(8,128)(2,1)} all-gather(bf16[256,128]{1,0:T(8,128)(2,1)S(1)} %copy-done.33), channel_id=1, replica_groups=mesh['dp'=8,'tensor'=4] {'dp'}, dimensions={1}, use_global_device_ids=true | all-gather | bytes 589824 | tf_op jit(solution)/shard_map/all_gather | solution.py:211
  57.1 4.8 while.38
  61.9 2.5 convolution_convert_fusion.3
  65.1 27.1 %reduce-scatter.11.cloned.1.call-done = bf16[128,1024]{1,0:T(8,128)(2,1)} async-done(((bf16[512,1024]{1,0:T(8,128)(2,1)}), bf16[128,1024]{1,0:T(8,128)(2,1)}) %reduce-scatter.11.cloned.1.call-update) | async-done | bytes 262160 | tf_op jit(solution)/shard_map/reduce_scatter | solution.py:221
  94.5 1.8 fusion.21
  97.6 27.1 %all-gather.9.cloned.1.call-done = bf16[512,1024]{1,0:T(8,128)(2,1)} async-done(((bf16[128,1024]{1,0:T(8,128)(2,1)}), bf16[512,1024]{1,0:T(8,128)(2,1)}) %all-gather.9.cloned.1.call-update) | async-done | bytes 1048592 | tf_op jit(solution)/shard_map/all_gather | solution.py:230
  124.7 4.6 multiply_convert_fusion.1
  129.3 24.4 %all-gather.13.cloned.1.call-done = bf16[1024,1024]{1,0:T(8,128)(2,1)} async-done(((bf16[1024,128]{1,0:T(8,128)(2,1)}), bf16[1024,1024]{1,0:T(8,128)(2,1)}) %all-gather.13.cloned.1.call-update) | async-done | bytes 2097168 | tf_op jit(solution)/shard_map/all_gather | solution.py:233
  153.8 3.9 convolution_convert_fusion.2
  157.7 27.4 %reduce-scatter.13.cloned.1.call-done = bf16[128,1024]{1,0:T(8,128)(2,1)} async-done(((bf16[512,1024]{1,0:T(8,128)(2,1)}), bf16[128,1024]{1,0:T(8,128)(2,1)}) %reduce-scatter.13.cloned.1.call-update) | async-done | bytes 262160 | tf_op jit(solution)/shard_map/reduce_scatter | solution.py:239
  188.3 26.4 %all-gather.15.cloned.1.call-done = bf16[512,1024]{1,0:T(8,128)(2,1)} async-done(((bf16[128,1024]{1,0:T(8,128)(2,1)}), bf16[512,1024]{1,0:T(8,128)(2,1)}) %all-gather.15.cloned.1.call-update) | async-done | bytes 1048592 | tf_op jit(solution)/shard_map/all_gather | solution.py:261
  214.7 5.2 fusion.37
  220.9 2.3 convolution_convert_fusion.1
  223.3 26.8 %reduce-scatter.15.cloned.1.call-done = bf16[128,1024]{1,0:T(8,128)(2,1)} async-done(((bf16[512,1024]{1,0:T(8,128)(2,1)}), bf16[128,1024]{1,0:T(8,128)(2,1)}) %reduce-scatter.15.cloned.1.call-update) | async-done | bytes 262160 | tf_op jit(solution)/shard_map/reduce_scatter | solution.py:267
  250.0 2.0 multiply_reduce_fusion.1
  252.0 1.8 fusion.32
  254.7 26.5 %all-gather.17.cloned.1.call-done = bf16[512,1024]{1,0:T(8,128)(2,1)} async-done(((bf16[128,1024]{1,0:T(8,128)(2,1)}), bf16[512,1024]{1,0:T(8,128)(2,1)}) %all-gather.17.cloned.1.call-update) | async-done | bytes 1048592 | tf_op jit(solution)/shard_map/all_gather | solution.py:281
  281.2 2.4 convolution_convert_fusion.4
  284.6 13.1 %while.39 = (s32[]{:T(128)}, f32[512,256]{0,1:T(8,128)}, f32[512,256]{0,1:T(8,128)S(1)}, f32[512,256]{0,1:T(8,128)S(1)}, bf16[512,256]{0,1:T(8,128)(2,1)S(1)}, /...) while((s32[]{:T(128)}, f32[512,256]{0,1:T(8,128)}, ...), condition=%wide.region_17.18_spmd.clone, body=%wide.region_15.17_spmd.clone.sunk | while | flops 340395520 | bytes 25846364 | solution.py:168
  297.7 2.9 convolution_bitcast_fusion.2
  309.5 4.5 fusion.41
  315.5 3.3 fusion.15
  321.4 41.4 %all-reduce = (f32[1024]{0:T(1024)}, f32[1024]{0:T(1024)}, f32[1024]{0:T(1024)}, f32[1024]{0:T(1024)}, f32[1024]{0:T(1024)}, /*index=5*/f32[4096]{0:T(1024)}, f32[1024]{0:T(1024)}, f32[1024]{0:T(1024)}, f32[1024]{0:T(1024)}) all-reduce(f32[1024]{0:T(1024)S(1)} %dynamic_update_slice.62, ...), channel_id=1, replica_groups=mesh['dp'=8,'tensor'=4] {'dp','tensor'}, use_global_device_ids=true, to_apply=%region_21.22 | all-reduce | flops 12288 | bytes 98304 | tf_op jit(solution)/shard_map/psum | solution.py:316
  364.4 10.7 %reduce-scatter.21.cloned.1.call-done = f32[128,256]{0,1:T(8,128)} async-done(((f32[1024,256]{0,1:T(8,128)}), f32[128,256]{0,1:T(8,128)}) %reduce-scatter.21.cloned.1.call-update) | async-done | bytes 131088 | tf_op jit(solution)/shard_map/reduce_scatter | solution.py:306
  376.8 37.3 %reduce-scatter.23.cloned.1.call-done = f32[128,256]{0,1:T(8,128)} async-done(((f32[1024,256]{0,1:T(8,128)}), f32[128,256]{0,1:T(8,128)}) %reduce-scatter.23.cloned.1.call-update) | async-done | bytes 131088 | tf_op jit(solution)/shard_map/reduce_scatter | solution.py:307
  415.8 27.8 %reduce-scatter.17.cloned.1.call-done = bf16[128,1024]{1,0:T(8,128)(2,1)} async-done(((bf16[512,1024]{1,0:T(8,128)(2,1)}), bf16[128,1024]{1,0:T(8,128)(2,1)}) %reduce-scatter.17.cloned.1.call-update) | async-done | bytes 262160 | tf_op jit(solution)/shard_map/reduce_scatter | solution.py:298
  445.4 36.2 %reduce-scatter.25.cloned.1.call-done = f32[256,128]{1,0:T(8,128)} async-done(((f32[256,1024]{1,0:T(8,128)}), f32[256,128]{1,0:T(8,128)}) %reduce-scatter.25.cloned.1.call-update) | async-done | bytes 131088 | tf_op jit(solution)/shard_map/reduce_scatter | solution.py:308
  481.6 54.9 %reduce-scatter.29.cloned.1.call-done = f32[1024,128]{1,0:T(8,128)} async-done(((f32[1024,1024]{1,0:T(8,128)}), f32[1024,128]{1,0:T(8,128)}) %reduce-scatter.29.cloned.1.call-update) | async-done | bytes 524304 | tf_op jit(solution)/shard_map/reduce_scatter | solution.py:275
  536.5 54.8 %reduce-scatter.27.cloned.1.call-done = f32[128,1024]{1,0:T(8,128)} async-done(((f32[1024,1024]{1,0:T(8,128)}), f32[128,1024]{1,0:T(8,128)}) %reduce-scatter.27.cloned.1.call-update) | async-done | bytes 524304 | tf_op jit(solution)/shard_map/reduce_scatter | solution.py:274
  (243 shorter events, 53.9 us)
Async XLA Ops:
  8.0 35.3 %copy-start.33 = (bf16[256,128]{1,0:T(8,128)(2,1)S(1)}, bf16[256,128]{1,0:T(8,128)(2,1)}, u32[]{:S(2)}) copy-start(bf16[256,128]{1,0:T(8,128)(2,1)} %param.29) | copy-start | bytes 196612
  8.0 45.8 %all-gather.7.cloned.1.call-start = ((), (), s32[]{:S(2)}) async-start(), calls=%async_computation.10 | async-start | bytes 1310720 | tf_op jit(solution)/shard_map/all_gather | solution.py:206
  8.8 83.4 %reduce-scatter.11.cloned.1.call-start = ((), (), s32[]{:S(2)}) async-start(), calls=%async_computation.11 | async-start | bytes 1310720 | tf_op jit(solution)/shard_map/reduce_scatter | solution.py:221
  24.6 31.2 %copy-start.16 = (bf16[1024,256]{1,0:T(8,128)(2,1)}, bf16[1024,256]{1,0:T(8,128)(2,1)S(1)}, u32[]{:S(2)}) copy-start(bf16[1024,256]{1,0:T(8,128)(2,1)S(1)} %all_gather.37) | copy-start | bytes 1572868
  34.1 22.2 %copy-start.19 = (bf16[1024,256]{1,0:T(8,128)(2,1)}, bf16[1024,256]{1,0:T(8,128)(2,1)S(1)}, u32[]{:S(2)}) copy-start(bf16[1024,256]{1,0:T(8,128)(2,1)S(1)} %all_gather.38) | copy-start | bytes 1572868
  61.8 30.3 %copy-start.2 = (bf16[128,1024]{1,0:T(8,128)(2,1)S(1)}, bf16[128,1024]{1,0:T(8,128)(2,1)}, u32[]{:S(2)}) copy-start(bf16[128,1024]{1,0:T(8,128)(2,1)} %param.22) | copy-start | bytes 786436
  61.9 30.3 %copy-start.31 = (f32[1024]{0:T(1024)S(1)}, f32[1024]{0:T(1024)}, u32[]{:S(2)}) copy-start(f32[1024]{0:T(1024)} %param.30) | copy-start | bytes 12292
  61.9 32.6 %copy-start.32 = (f32[1024]{0:T(1024)S(1)}, f32[1024]{0:T(1024)}, u32[]{:S(2)}) copy-start(f32[1024]{0:T(1024)} %param.31) | copy-start | bytes 12292
  61.9 32.6 %copy-start.34 = (f32[1024]{0:T(1024)S(1)}, f32[1024]{0:T(1024)}, u32[]{:S(2)}) copy-start(f32[1024]{0:T(1024)} %param.32) | copy-start | bytes 12292
  64.4 33.2 %all-gather.11.cloned.1.call-start = ((), (), s32[]{:S(2)}) async-start(), calls=%async_computation.13 | async-start | bytes 2359296 | tf_op jit(solution)/shard_map/all_gather | solution.py:232
  65.0 59.7 %all-gather.9.cloned.1.call-start = ((), (), s32[]{:S(2)}) async-start(), calls=%async_computation.12 | async-start | bytes 1310720 | tf_op jit(solution)/shard_map/all_gather | solution.py:230
  96.3 57.5 %all-gather.13.cloned.1.call-start = ((), (), s32[]{:S(2)}) async-start(), calls=%async_computation.14 | async-start | bytes 2359296 | tf_op jit(solution)/shard_map/all_gather | solution.py:233
  96.9 88.2 %reduce-scatter.13.cloned.1.call-start = ((), (), s32[]{:S(2)}) async-start(), calls=%async_computation.15 | async-start | bytes 1310720 | tf_op jit(solution)/shard_map/reduce_scatter | solution.py:239
  129.3 28.3 %copy-start.25 = (bf16[512,1024]{1,0:T(8,128)(2,1)}, bf16[512,1024]{1,0:T(8,128)(2,1)S(1)}, u32[]{:S(2)}) copy-start(bf16[512,1024]{1,0:T(8,128)(2,1)S(1)} %get-tuple-element.629) | copy-start | bytes 3145732
  153.8 31.3 %copy-start.11 = (bf16[128,1024]{1,0:T(8,128)(2,1)S(1)}, bf16[128,1024]{1,0:T(8,128)(2,1)}, u32[]{:S(2)}) copy-start(bf16[128,1024]{1,0:T(8,128)(2,1)} %reduce-scatter.11.cloned.1.call-done) | copy-start | bytes 786436
  153.8 31.3 %copy-start.40 = (f32[1024]{0:T(1024)S(1)}, f32[1024]{0:T(1024)}, u32[]{:S(2)}) copy-start(f32[1024]{0:T(1024)} %param.36) | copy-start | bytes 12292
  157.6 29.0 %copy-start.28 = (bf16[128,1024]{1,0:T(8,128)(2,1)S(1)}, bf16[128,1024]{1,0:T(8,128)(2,1)}, u32[]{:S(2)}) copy-start(bf16[128,1024]{1,0:T(8,128)(2,1)} %param.39) | copy-start | bytes 786436
  157.6 29.0 %copy-start.35 = (f32[1024]{0:T(1024)S(1)}, f32[1024]{0:T(1024)}, u32[]{:S(2)}) copy-start(f32[1024]{0:T(1024)} %param.37) | copy-start | bytes 12292
  157.6 29.4 %copy-start.41 = (f32[1024]{0:T(1024)S(1)}, f32[1024]{0:T(1024)}, u32[]{:S(2)}) copy-start(f32[1024]{0:T(1024)} %param.38) | copy-start | bytes 12292
  157.7 57.1 %all-gather.15.cloned.1.call-start = ((), (), s32[]{:S(2)}) async-start(), calls=%async_computation.16 | async-start | bytes 1310720 | tf_op jit(solution)/shard_map/all_gather | solution.py:261
  188.1 61.9 %reduce-scatter.15.cloned.1.call-start = ((), (), s32[]{:S(2)}) async-start(), calls=%async_computation.17 | async-start | bytes 1310720 | tf_op jit(solution)/shard_map/reduce_scatter | solution.py:267
  223.2 58.0 %all-gather.17.cloned.1.call-start = ((), (), s32[]{:S(2)}) async-start(), calls=%async_computation.18 | async-start | bytes 1310720 | tf_op jit(solution)/shard_map/all_gather | solution.py:281
  250.0 31.2 %copy-start.18 = (bf16[256,1024]{1,0:T(8,128)(2,1)S(1)}, bf16[256,1024]{1,0:T(8,128)(2,1)}, u32[]{:S(2)}) copy-start(bf16[256,1024]{1,0:T(8,128)(2,1)} %all_gather.40) | copy-start | bytes 1572868
  253.8 29.8 %copy-start.14 = (f32[128,1024]{1,0:T(8,128)}, f32[128,1024]{1,0:T(8,128)S(1)}, u32[]{:S(2)}) copy-start(f32[128,1024]{1,0:T(8,128)S(1)} %get-tuple-element.615) | copy-start | bytes 1572868
  254.7 108.1 %reduce-scatter.19.cloned.1.call-start = ((), (), s32[]{:S(2)}) async-start(), calls=%async_computation.20 | async-start | bytes 1179648 | tf_op jit(solution)/shard_map/reduce_scatter | solution.py:305
  300.6 74.5 %reduce-scatter.21.cloned.1.call-start = ((), (), s32[]{:S(2)}) async-start(), calls=%async_computation.21 | async-start | bytes 1179648 | tf_op jit(solution)/shard_map/reduce_scatter | solution.py:306
  302.2 111.9 %reduce-scatter.23.cloned.1.call-start = ((), (), s32[]{:S(2)}) async-start(), calls=%async_computation.22 | async-start | bytes 1179648 | tf_op jit(solution)/shard_map/reduce_scatter | solution.py:307
  303.7 139.8 %reduce-scatter.17.cloned.1.call-start = ((), (), s32[]{:S(2)}) async-start(), calls=%async_computation.19 | async-start | bytes 1310720 | tf_op jit(solution)/shard_map/reduce_scatter | solution.py:298
  307.9 173.7 %reduce-scatter.25.cloned.1.call-start = ((), (), s32[]{:S(2)}) async-start(), calls=%async_computation.23 | async-start | bytes 1179648 | tf_op jit(solution)/shard_map/reduce_scatter | solution.py:308
  309.4 227.1 %reduce-scatter.29.cloned.1.call-start = ((), (), s32[]{:S(2)}) async-start(), calls=%async_computation.25 | async-start | bytes 4718592 | tf_op jit(solution)/shard_map/reduce_scatter | solution.py:275
  314.0 277.3 %reduce-scatter.27.cloned.1.call-start = ((), (), s32[]{:S(2)}) async-start(), calls=%async_computation.24 | async-start | bytes 4718592 | tf_op jit(solution)/shard_map/reduce_scatter | solution.py:274
  318.8 124.8 %copy-start.15 = (f32[128,1024]{1,0:T(8,128)S(1)}, f32[128,1024]{1,0:T(8,128)}, u32[]{:S(2)}) copy-start(f32[128,1024]{1,0:T(8,128)} %copy-done.14) | copy-start | bytes 1572868
  (39 other events, 77.4 us)
Sparse Core Ops, SparseCore 0:
  10.4 30.6 all-gather.6
  64.5 27.5 reduce-scatter.10
  157.8 27.2 reduce-scatter.12
  188.2 26.4 all-gather.14
  223.3 26.6 reduce-scatter.14
Sparse Core Ops, SparseCore 1:
  66.8 27.9 all-gather.10
  96.8 27.9 all-gather.8
  126.4 27.3 all-gather.12
  254.7 26.4 all-gather.16
  300.7 35.2 reduce-scatter.18
  339.2 35.9 reduce-scatter.20
  378.2 35.9 reduce-scatter.22
  416.3 27.2 reduce-scatter.16
  447.2 34.3 reduce-scatter.24
  485.5 50.9 reduce-scatter.28
  540.3 50.9 reduce-scatter.26
where the time goes:
time: 600 us; the launch traced here: 599 us
  waiting for transfers between devices  409 us (68%)
  blocking collectives  82.3 us (14%)
  matrix products  48.7 us (8%)
  other arithmetic  21.4 us (4%)
  local copies, waits for them, and re-layouts  17.9 us (3%)
  between operations  17.3 us (3%)
    reduce_scatter x1, waiting for transfers between devices, on_device(): lax.psum_scatter(grad_w_back, 'dp', scatter_dimension=1, tiled=True)  54.9 us
    reduce_scatter x1, waiting for transfers between devices, on_device(): lax.psum_scatter(grad_w_in, 'dp', scatter_dimension=0, tiled=True)  54.8 us
    psum x1, blocking collectives, on_device(): lax.psum((widen(grad_b_query_part, b_query.shape[0]), widen(grad_b_value_...  41.4 us
    reduce_scatter x1, waiting for transfers between devices, on_device(): lax.psum_scatter(grad_w_value, 'dp', scatter_dimension=0, tiled=True)  37.3 us
    reduce_scatter x1, waiting for transfers between devices, on_device(): lax.psum_scatter(grad_w_out, 'dp', scatter_dimension=1, tiled=True)  36.2 us
    reduce_scatter x1, waiting for transfers between devices, on_device(): lax.psum_scatter((query_part + key_part + value_part).astype(jnp.bfloat16...  27.8 us
    reduce_scatter x1, waiting for transfers between devices, on_device(): lax.psum_scatter(matmul_plain(activation, mat_back).astype(jnp.bfloat16),...  27.4 us
    reduce_scatter x1, waiting for transfers between devices, on_device(): lax.psum_scatter(matmul_plain(context, mat_out).astype(jnp.bfloat16), 'te...  27.1 us
  transfers between devices with their start and end apart: 16, of which 13 were waited for; matrix products, arithmetic and copies ran while one was open for 6% of the time, Pallas kernels for 0%

commit v1 on v0

--- a/solution.py
+++ b/solution.py
@@ -227,7 +227,23 @@
     resid_one = tokens.astype(jnp.float32) + attn_sum + b_out
     hidden_one, normed_one, inv_one = layer_norm(resid_one, gain_attn, shift_attn)
     hidden_bf = hidden_one.astype(jnp.bfloat16)
-    hidden_full = lax.all_gather(hidden_bf, "tensor", axis=0, tiled=True)
+    ways, here, turn = (lax.axis_size("tensor"), lax.axis_index("tensor"), hidden_bf.shape[0])
+    dims = [n * ways if d == 0 else n for d, n in enumerate(hidden_bf.shape)]
+    full = lax.dynamic_update_slice_in_dim(
+        jnp.zeros(dims, hidden_bf.dtype), hidden_bf, here * turn, axis=0
+    )
+    going_up = going_down = hidden_bf
+    for far in range(1, ways // 2 + 1):
+        going_up = lax.ppermute(going_up, "tensor", [(d, (d + 1) % ways) for d in range(ways)])
+        full = lax.dynamic_update_slice_in_dim(full, going_up, (here - far) % ways * turn, axis=0)
+        if 2 * far < ways:
+            going_down = lax.ppermute(
+                going_down, "tensor", [(d, (d - 1) % ways) for d in range(ways)]
+            )
+            full = lax.dynamic_update_slice_in_dim(
+                full, going_down, (here + far) % ways * turn, axis=0
+            )
+    hidden_full = full
     ffn_mats = (
         lax.all_gather(w_in, "dp", axis=0, tiled=True),
         lax.all_gather(w_back, "dp", axis=1, tiled=True),

time: 600 us -> 572 us (0.953)
  waiting for transfers between devices: 409 us -> 375 us
    all_gather x1 -> x0, waiting for transfers between devices: 27.1 us -> none  [on_device(): hidden_full = lax.all_gather(hidden_bf, 'tensor', axis=0, tiled=True)]
    all_gather x1, waiting for transfers between devices: 24.4 us -> 3.77 us  [on_device(): lax.all_gather(w_back, 'dp', axis=1, tiled=True)]
    ppermute x0 -> x3, waiting for transfers between devices: none -> 15.2 us  [the longest x2 13.5 us: on_device(): lax.ppermute(going_up, 'tensor', [(d, (d + 1) % ways) for d in range(ways)])]
  transfers between devices with their start and end apart: 16 -> 18, of which waited for: 13 -> 15; matrix products, arithmetic and copies ran while one was open for 6% -> 7% of each run, Pallas kernels for 0% -> 0%
where the time goes in v1:
time: 572 us; the launch traced here: 571 us
  waiting for transfers between devices  375 us (66%)
  blocking collectives  82.4 us (14%)
  matrix products  52 us (9%)
  local copies, waits for them, and re-layouts  19 us (3%)
  other arithmetic  18.7 us (3%)
  between operations  17.6 us (3%)
    reduce_scatter x1, waiting for transfers between devices, on_device(): lax.psum_scatter(grad_w_in, 'dp', scatter_dimension=0, tiled=True)  54.8 us
    reduce_scatter x1, waiting for transfers between devices, on_device(): lax.psum_scatter(grad_w_back, 'dp', scatter_dimension=1, tiled=True)  54.7 us
    psum x1, blocking collectives, on_device(): lax.psum((widen(grad_b_query_part, b_query.shape[0]), widen(grad_b_value_...  41.5 us
    reduce_scatter x1, waiting for transfers between devices, on_device(): lax.psum_scatter(grad_w_value, 'dp', scatter_dimension=0, tiled=True)  37.5 us
    reduce_scatter x1, waiting for transfers between devices, on_device(): lax.psum_scatter(grad_w_out, 'dp', scatter_dimension=1, tiled=True)  36.2 us
    reduce_scatter x1, waiting for transfers between devices, on_device(): lax.psum_scatter((query_part + key_part + value_part).astype(jnp.bfloat16...  27.9 us
    reduce_scatter x1, waiting for transfers between devices, on_device(): lax.psum_scatter(matmul_plain(activation, mat_back).astype(jnp.bfloat16),...  27.4 us
    reduce_scatter x1, waiting for transfers between devices, on_device(): lax.psum_scatter(matmul_over_cols(grad_pre_bf, mat_in).astype(jnp.bfloat1...  26.8 us
  transfers between devices with their start and end apart: 18, of which 15 were waited for; matrix products, arithmetic and copies ran while one was open for 7% of the time, Pallas kernels for 0%

profile of v1, /device:TPU:0, one launch (start us, length us, event | category | flops | bytes accessed | tf_op | source)
XLA Modules:
  0.0 570.5 jit_solution(16705907828952187201)
XLA Ops:
  13.0 11.6 %all_gather.34 = bf16[1024,256]{1,0:T(8,128)(2,1)S(1)} all-gather(bf16[128,256]{1,0:T(8,128)(2,1)} %param.27), channel_id=1, replica_groups=mesh['dp'=8,'tensor'=4] {'dp'}, dimensions={0}, use_global_device_ids=true | all-gather | bytes 589824 | tf_op jit(solution)/shard_map/all_gather | solution.py:210
  24.6 9.5 %all_gather.35 = bf16[1024,256]{1,0:T(8,128)(2,1)S(1)} all-gather(bf16[128,256]{1,0:T(8,128)(2,1)} %param.24), channel_id=1, replica_groups=mesh['dp'=8,'tensor'=4] {'dp'}, dimensions={0}, use_global_device_ids=true | all-gather | bytes 589824 | tf_op jit(solution)/shard_map/all_gather | solution.py:208
  34.1 9.2 %all_gather.36 = bf16[1024,256]{1,0:T(8,128)(2,1)S(1)} all-gather(bf16[128,256]{1,0:T(8,128)(2,1)} %param.26), channel_id=1, replica_groups=mesh['dp'=8,'tensor'=4] {'dp'}, dimensions={0}, use_global_device_ids=true | all-gather | bytes 589824 | tf_op jit(solution)/shard_map/all_gather | solution.py:209
  43.3 10.6 %all_gather.37 = bf16[256,1024]{1,0:T(8,128)(2,1)} all-gather(bf16[256,128]{1,0:T(8,128)(2,1)S(1)} %copy-done.33), channel_id=1, replica_groups=mesh['dp'=8,'tensor'=4] {'dp'}, dimensions={1}, use_global_device_ids=true | all-gather | bytes 589824 | tf_op jit(solution)/shard_map/all_gather | solution.py:211
  57.0 4.8 while.38
  61.9 2.5 convolution_convert_fusion.3
  65.6 26.5 %reduce-scatter.11.cloned.1.call-done = bf16[128,1024]{1,0:T(8,128)(2,1)} async-done(((bf16[512,1024]{1,0:T(8,128)(2,1)}), bf16[128,1024]{1,0:T(8,128)(2,1)}) %reduce-scatter.11.cloned.1.call-update) | async-done | bytes 262160 | tf_op jit(solution)/shard_map/reduce_scatter | solution.py:221
  94.9 3.8 collective-permute-start.1
  98.7 7.2 %collective-permute-done = bf16[128,1024]{1,0:T(8,128)(2,1)S(1)} collective-permute-done((bf16[128,1024]{1,0:T(8,128)(2,1)S(1)}, bf16[128,1024]{1,0:T(8,128)(2,1)S(1)}, u32[]{:S(2)}, u32[]{:S(2)}) %collective-permute-start) | collective-permute-done | bytes 262176 | tf_op jit(solution)/shard_map/ppermute | solution.py:237
  109.3 6.3 %collective-permute-done.2 = bf16[128,1024]{1,0:T(8,128)(2,1)S(1)} collective-permute-done((bf16[128,1024]{1,0:T(8,128)(2,1)S(1)}, bf16[128,1024]{1,0:T(8,128)(2,1)S(1)}, u32[]{:S(2)}, u32[]{:S(2)}) %collective-permute-start.2) | collective-permute-done | bytes 262176 | tf_op jit(solution)/shard_map/ppermute | solution.py:237
  115.7 5.0 multiply_convert_fusion.1
  120.7 3.8 all-gather.10.cloned.1.call-done
  124.5 4.2 convolution_convert_fusion.2
  128.8 27.4 %reduce-scatter.13.cloned.1.call-done = bf16[128,1024]{1,0:T(8,128)(2,1)} async-done(((bf16[512,1024]{1,0:T(8,128)(2,1)}), bf16[128,1024]{1,0:T(8,128)(2,1)}) %reduce-scatter.13.cloned.1.call-update) | async-done | bytes 262160 | tf_op jit(solution)/shard_map/reduce_scatter | solution.py:255
  159.4 26.4 %all-gather.12.cloned.1.call-done = bf16[512,1024]{1,0:T(8,128)(2,1)} async-done(((bf16[128,1024]{1,0:T(8,128)(2,1)}), bf16[512,1024]{1,0:T(8,128)(2,1)}) %all-gather.12.cloned.1.call-update) | async-done | bytes 1048592 | tf_op jit(solution)/shard_map/all_gather | solution.py:277
  185.8 5.2 fusion.32
  191.9 2.3 convolution_convert_fusion.1
  194.3 26.8 %reduce-scatter.15.cloned.1.call-done = bf16[128,1024]{1,0:T(8,128)(2,1)} async-done(((bf16[512,1024]{1,0:T(8,128)(2,1)}), bf16[128,1024]{1,0:T(8,128)(2,1)}) %reduce-scatter.15.cloned.1.call-update) | async-done | bytes 262160 | tf_op jit(solution)/shard_map/reduce_scatter | solution.py:283
  225.7 26.6 %all-gather.14.cloned.1.call-done = bf16[512,1024]{1,0:T(8,128)(2,1)} async-done(((bf16[128,1024]{1,0:T(8,128)(2,1)}), bf16[512,1024]{1,0:T(8,128)(2,1)}) %all-gather.14.cloned.1.call-update) | async-done | bytes 1048592 | tf_op jit(solution)/shard_map/all_gather | solution.py:297
  252.3 2.4 convolution_convert_fusion.4
  255.7 13.3 %while.39 = (s32[]{:T(128)}, f32[512,256]{0,1:T(8,128)}, f32[512,256]{0,1:T(8,128)S(1)}, f32[512,256]{0,1:T(8,128)S(1)}, bf16[512,256]{0,1:T(8,128)(2,1)S(1)}, /...) while((s32[]{:T(128)}, f32[512,256]{0,1:T(8,128)}, ...), condition=%wide.region_17.18_spmd.clone, body=%wide.region_15.17_spmd.clone.sunk | while | flops 340395520 | bytes 30040732 | solution.py:168
  269.1 2.9 convolution_bitcast_fusion.2
  279.3 2.8 fusion.42
  282.1 4.5 fusion.15
  287.9 4.5 fusion.43
  294.0 41.5 %all-reduce = (f32[1024]{0:T(1024)}, f32[1024]{0:T(1024)}, f32[1024]{0:T(1024)}, f32[1024]{0:T(1024)}, f32[1024]{0:T(1024)}, /*index=5*/f32[4096]{0:T(1024)}, f32[1024]{0:T(1024)}, f32[1024]{0:T(1024)}, f32[1024]{0:T(1024)}) all-reduce(f32[1024]{0:T(1024)S(1)} %dynamic_update_slice.78, ...), channel_id=1, replica_groups=mesh['dp'=8,'tensor'=4] {'dp','tensor'}, use_global_device_ids=true, to_apply=%region_21.22 | all-reduce | flops 12288 | bytes 98304 | tf_op jit(solution)/shard_map/psum | solution.py:332
  337.1 9.5 %reduce-scatter.21.cloned.1.call-done = f32[128,256]{0,1:T(8,128)} async-done(((f32[1024,256]{0,1:T(8,128)}), f32[128,256]{0,1:T(8,128)}) %reduce-scatter.21.cloned.1.call-update) | async-done | bytes 131088 | tf_op jit(solution)/shard_map/reduce_scatter | solution.py:322
  348.3 37.5 %reduce-scatter.23.cloned.1.call-done = f32[128,256]{0,1:T(8,128)} async-done(((f32[1024,256]{0,1:T(8,128)}), f32[128,256]{0,1:T(8,128)}) %reduce-scatter.23.cloned.1.call-update) | async-done | bytes 131088 | tf_op jit(solution)/shard_map/reduce_scatter | solution.py:323
  387.4 27.9 %reduce-scatter.17.cloned.1.call-done = bf16[128,1024]{1,0:T(8,128)(2,1)} async-done(((bf16[512,1024]{1,0:T(8,128)(2,1)}), bf16[128,1024]{1,0:T(8,128)(2,1)}) %reduce-scatter.17.cloned.1.call-update) | async-done | bytes 262160 | tf_op jit(solution)/shard_map/reduce_scatter | solution.py:314
  417.1 36.2 %reduce-scatter.25.cloned.1.call-done = f32[256,128]{1,0:T(8,128)} async-done(((f32[256,1024]{1,0:T(8,128)}), f32[256,128]{1,0:T(8,128)}) %reduce-scatter.25.cloned.1.call-update) | async-done | bytes 131088 | tf_op jit(solution)/shard_map/reduce_scatter | solution.py:324
  453.4 54.8 %reduce-scatter.27.cloned.1.call-done = f32[128,1024]{1,0:T(8,128)} async-done(((f32[1024,1024]{1,0:T(8,128)}), f32[128,1024]{1,0:T(8,128)}) %reduce-scatter.27.cloned.1.call-update) | async-done | bytes 524304 | tf_op jit(solution)/shard_map/reduce_scatter | solution.py:290
  508.2 54.7 %reduce-scatter.29.cloned.1.call-done = f32[1024,128]{1,0:T(8,128)} async-done(((f32[1024,1024]{1,0:T(8,128)}), f32[1024,128]{1,0:T(8,128)}) %reduce-scatter.29.cloned.1.call-update) | async-done | bytes 524304 | tf_op jit(solution)/shard_map/reduce_scatter | solution.py:291
  (254 shorter events, 58.3 us)
Async XLA Ops:
  8.0 35.3 %copy-start.33 = (bf16[256,128]{1,0:T(8,128)(2,1)S(1)}, bf16[256,128]{1,0:T(8,128)(2,1)}, u32[]{:S(2)}) copy-start(bf16[256,128]{1,0:T(8,128)(2,1)} %param.29) | copy-start | bytes 196612
  8.0 45.8 %all-gather.6.cloned.1.call-start = ((), (), s32[]{:S(2)}) async-start(), calls=%async_computation.10 | async-start | bytes 1310720 | tf_op jit(solution)/shard_map/all_gather | solution.py:206
  8.8 83.4 %reduce-scatter.11.cloned.1.call-start = ((), (), s32[]{:S(2)}) async-start(), calls=%async_computation.11 | async-start | bytes 1310720 | tf_op jit(solution)/shard_map/reduce_scatter | solution.py:221
  24.6 31.2 %copy-start.21 = (bf16[1024,256]{1,0:T(8,128)(2,1)}, bf16[1024,256]{1,0:T(8,128)(2,1)S(1)}, u32[]{:S(2)}) copy-start(bf16[1024,256]{1,0:T(8,128)(2,1)S(1)} %all_gather.34) | copy-start | bytes 1572868
  34.1 21.7 %copy-start.26 = (bf16[1024,256]{1,0:T(8,128)(2,1)}, bf16[1024,256]{1,0:T(8,128)(2,1)S(1)}, u32[]{:S(2)}) copy-start(bf16[1024,256]{1,0:T(8,128)(2,1)S(1)} %all_gather.35) | copy-start | bytes 1572868
  61.8 30.3 %copy-start.2 = (bf16[128,1024]{1,0:T(8,128)(2,1)S(1)}, bf16[128,1024]{1,0:T(8,128)(2,1)}, u32[]{:S(2)}) copy-start(bf16[128,1024]{1,0:T(8,128)(2,1)} %param.22) | copy-start | bytes 786436
  61.9 30.3 %copy-start.31 = (f32[1024]{0:T(1024)S(1)}, f32[1024]{0:T(1024)}, u32[]{:S(2)}) copy-start(f32[1024]{0:T(1024)} %param.30) | copy-start | bytes 12292
  64.4 30.3 %copy-start.32 = (f32[1024]{0:T(1024)S(1)}, f32[1024]{0:T(1024)}, u32[]{:S(2)}) copy-start(f32[1024]{0:T(1024)} %param.31) | copy-start | bytes 12292
  64.4 30.3 %copy-start.34 = (f32[1024]{0:T(1024)S(1)}, f32[1024]{0:T(1024)}, u32[]{:S(2)}) copy-start(f32[1024]{0:T(1024)} %param.32) | copy-start | bytes 12292
  64.4 51.3 %all-gather.8.cloned.1.call-start = ((), (), s32[]{:S(2)}) async-start(), calls=%async_computation.12 | async-start | bytes 2359296 | tf_op jit(solution)/shard_map/all_gather | solution.py:248
  65.0 59.5 %all-gather.10.cloned.1.call-start = ((), (), s32[]{:S(2)}) async-start(), calls=%async_computation.13 | async-start | bytes 2359296 | tf_op jit(solution)/shard_map/all_gather | solution.py:249
  65.6 90.5 %reduce-scatter.13.cloned.1.call-start = ((), (), s32[]{:S(2)}) async-start(), calls=%async_computation.14 | async-start | bytes 1310720 | tf_op jit(solution)/shard_map/reduce_scatter | solution.py:255
  94.9 11.0 %collective-permute-start = (bf16[128,1024]{1,0:T(8,128)(2,1)S(1)}, bf16[128,1024]{1,0:T(8,128)(2,1)S(1)}, u32[]{:S(2)}, u32[]{:S(2)}) collective-permute-start(bf16[128,1024]{1,0:T(8,128)(2,1)S(1)} %get-tuple-element.623), channel_id=1, source_target_pairs={{0,1},{1,2},{2,3},{3,0},{4,5},{5,6},{6,7},{7,4},{8,9},{9,10},{10,1... | collective-permute-start | bytes 786440 | tf_op jit(solution)/shard_map/ppermute | solution.py:237
  94.9 13.4 %collective-permute-start.1 = (bf16[128,1024]{1,0:T(8,128)(2,1)S(1)}, bf16[128,1024]{1,0:T(8,128)(2,1)}, u32[]{:S(2)}, u32[]{:S(2)}) collective-permute-start(bf16[128,1024]{1,0:T(8,128)(2,1)S(1)} %get-tuple-element.623), channel_id=1, source_target_pairs={{0,3},{1,0},{2,1},{3,2},{4,7},{5,4},{6,5},{7,6},{8,11},{9,8},{10,9... | collective-permute-start | bytes 786440 | tf_op jit(solution)/shard_map/ppermute | solution.py:240
  105.9 9.8 %collective-permute-start.2 = (bf16[128,1024]{1,0:T(8,128)(2,1)S(1)}, bf16[128,1024]{1,0:T(8,128)(2,1)S(1)}, u32[]{:S(2)}, u32[]{:S(2)}) collective-permute-start(bf16[128,1024]{1,0:T(8,128)(2,1)S(1)} %collective-permute-done), channel_id=1, source_target_pairs={{0,1},{1,2},{2,3},{3,0},{4,5},{5,6},{6,7},{7,4},{8,9},{9,10},{10,1... | collective-permute-start | bytes 786440 | tf_op jit(solution)/shard_map/ppermute | solution.py:237
  124.5 31.6 %copy-start.40 = (f32[1024]{0:T(1024)S(1)}, f32[1024]{0:T(1024)}, u32[]{:S(2)}) copy-start(f32[1024]{0:T(1024)} %param.36) | copy-start | bytes 12292
  128.7 29.0 %copy-start.29 = (bf16[128,1024]{1,0:T(8,128)(2,1)S(1)}, bf16[128,1024]{1,0:T(8,128)(2,1)}, u32[]{:S(2)}) copy-start(bf16[128,1024]{1,0:T(8,128)(2,1)} %param.39) | copy-start | bytes 786436
  128.7 29.0 %copy-start.35 = (f32[1024]{0:T(1024)S(1)}, f32[1024]{0:T(1024)}, u32[]{:S(2)}) copy-start(f32[1024]{0:T(1024)} %param.37) | copy-start | bytes 12292
  128.7 29.3 %copy-start.41 = (f32[1024]{0:T(1024)S(1)}, f32[1024]{0:T(1024)}, u32[]{:S(2)}) copy-start(f32[1024]{0:T(1024)} %param.38) | copy-start | bytes 12292
  128.7 57.1 %all-gather.12.cloned.1.call-start = ((), (), s32[]{:S(2)}) async-start(), calls=%async_computation.15 | async-start | bytes 1310720 | tf_op jit(solution)/shard_map/all_gather | solution.py:277
  159.1 62.0 %reduce-scatter.15.cloned.1.call-start = ((), (), s32[]{:S(2)}) async-start(), calls=%async_computation.16 | async-start | bytes 1310720 | tf_op jit(solution)/shard_map/reduce_scatter | solution.py:283
  194.3 58.1 %all-gather.14.cloned.1.call-start = ((), (), s32[]{:S(2)}) async-start(), calls=%async_computation.17 | async-start | bytes 1310720 | tf_op jit(solution)/shard_map/all_gather | solution.py:297
  221.1 31.2 %copy-start.23 = (bf16[256,1024]{1,0:T(8,128)(2,1)S(1)}, bf16[256,1024]{1,0:T(8,128)(2,1)}, u32[]{:S(2)}) copy-start(bf16[256,1024]{1,0:T(8,128)(2,1)} %all_gather.37) | copy-start | bytes 1572868
  224.9 29.9 %copy-start.19 = (f32[128,1024]{1,0:T(8,128)}, f32[128,1024]{1,0:T(8,128)S(1)}, u32[]{:S(2)}) copy-start(f32[128,1024]{1,0:T(8,128)S(1)} %get-tuple-element.617) | copy-start | bytes 1572868
  225.7 109.7 %reduce-scatter.19.cloned.1.call-start = ((), (), s32[]{:S(2)}) async-start(), calls=%async_computation.19 | async-start | bytes 1179648 | tf_op jit(solution)/shard_map/reduce_scatter | solution.py:321
  272.0 74.7 %reduce-scatter.21.cloned.1.call-start = ((), (), s32[]{:S(2)}) async-start(), calls=%async_computation.20 | async-start | bytes 1179648 | tf_op jit(solution)/shard_map/reduce_scatter | solution.py:322
  273.5 112.2 %reduce-scatter.23.cloned.1.call-start = ((), (), s32[]{:S(2)}) async-start(), calls=%async_computation.21 | async-start | bytes 1179648 | tf_op jit(solution)/shard_map/reduce_scatter | solution.py:323
  275.1 140.2 %reduce-scatter.17.cloned.1.call-start = ((), (), s32[]{:S(2)}) async-start(), calls=%async_computation.18 | async-start | bytes 1310720 | tf_op jit(solution)/shard_map/reduce_scatter | solution.py:314
  279.3 174.1 %reduce-scatter.25.cloned.1.call-start = ((), (), s32[]{:S(2)}) async-start(), calls=%async_computation.22 | async-start | bytes 1179648 | tf_op jit(solution)/shard_map/reduce_scatter | solution.py:324
  282.1 226.1 %reduce-scatter.27.cloned.1.call-start = ((), (), s32[]{:S(2)}) async-start(), calls=%async_computation.23 | async-start | bytes 4718592 | tf_op jit(solution)/shard_map/reduce_scatter | solution.py:290
  286.7 276.2 %reduce-scatter.29.cloned.1.call-start = ((), (), s32[]{:S(2)}) async-start(), calls=%async_computation.24 | async-start | bytes 4718592 | tf_op jit(solution)/shard_map/reduce_scatter | solution.py:291
  292.4 122.9 %copy-start.20 = (f32[128,1024]{1,0:T(8,128)S(1)}, f32[128,1024]{1,0:T(8,128)}, u32[]{:S(2)}) copy-start(f32[128,1024]{1,0:T(8,128)} %copy-done.19) | copy-start | bytes 1572868
  (43 other events, 80.6 us)
Sparse Core Ops, SparseCore 0:
  10.4 30.6 all-gather.5
  64.5 27.5 reduce-scatter.10
  128.8 27.2 reduce-scatter.12
  159.3 26.4 all-gather.11
  194.4 26.6 reduce-scatter.14
  225.8 26.4 all-gather.13
Sparse Core Ops, SparseCore 1:
  66.8 27.9 all-gather.7
  96.5 27.9 all-gather.9
  272.0 35.2 reduce-scatter.18
  310.5 36.0 reduce-scatter.20
  349.8 35.9 reduce-scatter.22
  388.1 27.2 reduce-scatter.16
  418.9 34.4 reduce-scatter.24
  457.2 50.9 reduce-scatter.26
  512.0 50.9 reduce-scatter.28
